TPU v7x, 32 devices: a whole 2x2x4 slice. The times are simulated.
32 devices in a mesh: row: 8 (over z, core), col: 4 (over y, x).
Axes of the slice: x: 2, y: 2, z: 4, core: 2. Of those that a mesh axis runs over, the one named last changes fastest.
Arguments:
- loadings: bfloat16 [8, 32768, 1024], P(None, 'row', 'col'), may hold values from -6 to 6
- weights: bfloat16 [8, 32768, 512], P(None, 'row', 'col'), may hold values from -0.03125 to 0.03125
- specific: float32 [8, 32768], P(None, 'row'), may hold values from 0.2 to 5
- factor_cov: float32 [8, 1024, 1024], P(None, 'col'), may hold values from -0.001953125 to 0.0048828125, as said below
Outputs:
- portfolio_cov: float32 [8, 512, 512], P(None, 'row', 'col')
Inputs may be any that keep to these rules, and one draw needn't show every extreme that they name: `factor_cov`: each day's matrix is a symmetric positive definite factor covariance of order 1024.
All inputs are finite; a program needn't handle non-finite values.
Results may differ from a plain program's by a relative error of at most 0.0003.
Values may be sent and summed in bfloat16 or wider, within the bound.
A program may use at most 128 MiB of HBM per device.

v0:
```python
import jax
import jax.numpy as jnp
from jax import lax
from jax.sharding import PartitionSpec as P


def shards(loadings, weights, specific, factor_cov):
    factor_cols = loadings.shape[2]
    port_cols = weights.shape[2]
    total_ports = port_cols * lax.axis_size("col")
    port_rows = total_ports // lax.axis_size("row")
    row_start = lax.axis_index("row") * port_rows
    weighted = (specific[:, :, None] * weights.astype(jnp.float32)).astype(jnp.bfloat16)
    fragment = lax.all_gather(weights, "col", axis=2, tiled=True)
    exposure_part = jnp.einsum(
        "dar,dap->drp", loadings, fragment, preferred_element_type=jnp.float32
    )
    specific_term = jnp.einsum(
        "dak,dap->dkp", weighted, fragment, preferred_element_type=jnp.float32
    )
    joined = jnp.concatenate([exposure_part, specific_term], axis=1)
    exposure = lax.psum(joined[:, :factor_cols, :], "row")
    specific_block = lax.psum_scatter(
        joined[:, factor_cols:, :], "row", scatter_dimension=2, tiled=True
    )
    exposure_rows = lax.dynamic_slice_in_dim(exposure, row_start, port_rows, 2)
    left_part = jnp.einsum(
        "dri,drs->dis", exposure_rows, factor_cov, precision=lax.Precision.HIGHEST
    )
    left = lax.psum(left_part, "col")
    exposure_cols = lax.all_to_all(exposure, "col", split_axis=2, concat_axis=1, tiled=True)
    factor_block = jnp.einsum("dir,drk->dik", left, exposure_cols, precision=lax.Precision.HIGHEST)
    return factor_block + jnp.swapaxes(specific_block, 1, 2)


def solution(mesh):
    in_specs = (P(None, "row", "col"), P(None, "row", "col"), P(None, "row"), P(None, "col", None))
    out_specs = P(None, "row", "col")
    return jax.shard_map(shards, mesh=mesh, in_specs=in_specs, out_specs=out_specs, check_vma=False)
```

profile of v0, /device:TPU:0, one launch (start us, length us, event | category | flops | bytes accessed | tf_op | source)
XLA Modules:
  0.0 558.4 jit_solution(18040227865551506382)
XLA Ops:
  6.5 0.0 all-gather.2.cloned.1.call-start
  6.5 0.7 all-gather.2.cloned.1.call-update
  7.3 0.0 copy-start
  7.3 0.0 all-reduce.3.cloned.1.call-start
  7.3 301.6 %all-gather.2.cloned.1.call-done = bf16[8,4096,512]{2,1,0:T(8,128)(2,1)} async-done(((bf16[8,4096,128]{2,1,0:T(8,128)(2,1)}), bf16[8,4096,512]{2,1,0:T(8,128)(2,1)}) %all-gather.2.cloned.1.call-update) | async-done | bytes 33554448 | tf_op jit(solution)/shard_map/all_gather | solution.py:14
  308.9 21.1 %fusion.5 = f32[8,256,512]{2,1,0:T(8,128)} fusion(bf16[8,4096,256]{2,1,0:T(8,128)(2,1)} %param.4, bf16[8,4096,512]{2,1,0:T(8,128)(2,1)} %all-gather.2.cloned.1.call-done), kind=kOutput, calls=%fused_computation.7 | convolution fusion | flops 8589934592 | bytes 54525952 | tf_op jit(solution)/shard_map/dar,dap->drp/dot_general | solution.py:15
  329.9 0.0 all-reduce.3.cloned.1.call-update
  330.0 0.0 reduce-scatter.2.cloned.1.call-start
  330.0 0.0 copy-done
  330.0 21.5 %fusion = f32[8,128,512]{1,2,0:T(8,128)} fusion(bf16[8,4096,512]{2,1,0:T(8,128)(2,1)} %all-gather.2.cloned.1.call-done, bf16[8,4096,128]{2,1,0:T(8,128)(2,1)} %param.5, f32[8,4096]{1,0:T(8,128)S(1)} %copy-done), kind=kOutput, calls=%fused_computation.1 | convolution fusion | flops 4307550208 | bytes 44171264 | tf_op jit(solution)/shard_map/dak,dap->dkp/dot_general | solution.py:18
  351.5 0.0 reduce-scatter.2.cloned.1.call-update
  351.5 75.1 %all-reduce.3.cloned.1.call-done = f32[8,256,512]{2,1,0:T(8,128)} async-done(((f32[8,256,512]{2,1,0:T(8,128)}), f32[8,256,512]{2,1,0:T(8,128)}) %all-reduce.3.cloned.1.call-update) | async-done | bytes 4194320 | tf_op jit(solution)/shard_map/psum | solution.py:22
  426.6 5.5 copy.9
  432.1 5.0 all-to-all-start
  437.1 0.2 all-reduce.5.cloned.1.call-start
  437.3 10.4 %fusion.2 = f32[8,64,1024]{2,1,0:T(8,128)} fusion(f32[8,256,1024]{2,1,0:T(8,128)} %param.7, f32[8,256,512]{2,1,0:T(8,128)} %all-reduce.3.cloned.1.call-done, s32[]{:T(128)S(6)} %select_n.3), kind=kOutput, calls=%fused_computation.4 | convolution fusion | flops 1610612736 | bytes 11534340 | tf_op jit(solution)/shard_map/dri,drs->dis/dot_general | solution.py:27
  447.7 0.0 all-reduce.5.cloned.1.call-update
  447.7 47.9 %all-to-all-done = f32[8,256,512]{1,0,2:T(8,128)} async-done(((f32[8,256,512]{1,0,2:T(8,128)}), f32[8,256,512]{1,0,2:T(8,128)}, u32[]{:S(2)}, u32[]{:S(2)}) %all-to-all-start) | async-done | bytes 4194336 | tf_op jit(solution)/shard_map/all_to_all | solution.py:31
  495.6 5.3 copy.10
  500.9 0.0 reduce-scatter.2.cloned.1.call-done
  500.9 44.7 %all-reduce.5.cloned.1.call-done = f32[8,64,1024]{2,1,0:T(8,128)} async-done(((f32[8,64,1024]{2,1,0:T(8,128)}), f32[8,64,1024]{2,1,0:T(8,128)}) %all-reduce.5.cloned.1.call-update) | async-done | bytes 2097168 | tf_op jit(solution)/shard_map/psum | solution.py:30
  545.7 6.2 %convolution_add_fusion = f32[8,64,128]{2,1,0:T(8,128)} fusion(f32[8,64,1024]{2,1,0:T(8,128)} %all-reduce.5.cloned.1.call-done, f32[8,1024,128]{2,1,0:T(8,128)} %bitcast.12, f32[8,128,64]{1,2,0:T(8,128)} %reduce-scatter.2.cloned.1.call-done), kind=kOutput, calls=%fused_computation.3 | convolution fusion | flops 805371904 | bytes 6815744 | tf_op jit(solution)/shard_map/dir,drk->dik/dot_general | solution.py:32
Async XLA Ops:
  6.5 302.3 %all-gather.2.cloned.1.call-start = ((), (), s32[]{:S(2)}) async-start(), calls=%async_computation.2 | async-start | bytes 41943040 | tf_op jit(solution)/shard_map/all_gather | solution.py:14
  7.3 322.8 %copy-start = (f32[8,4096]{1,0:T(8,128)S(1)}, f32[8,4096]{1,0:T(8,128)}, u32[]{:S(2)}) copy-start(f32[8,4096]{1,0:T(8,128)} %param.6) | copy-start | bytes 393220
  7.3 419.3 %all-reduce.3.cloned.1.call-start = ((), (), s32[]{:S(2)}) async-start(), calls=%async_computation.3 | async-start | bytes 8388608 | tf_op jit(solution)/shard_map/psum | solution.py:22
  330.0 171.0 %reduce-scatter.2.cloned.1.call-start = ((), (), s32[]{:S(2)}) async-start(), calls=%async_computation.5 | async-start | bytes 2359296 | tf_op jit(solution)/shard_map/reduce_scatter | solution.py:23
  432.1 63.5 %all-to-all-start = ((f32[8,256,512]{1,0,2:T(8,128)}), f32[8,256,512]{1,0,2:T(8,128)}, u32[]{:S(2)}, u32[]{:S(2)}) async-start(f32[8,256,512]{1,0,2:T(8,128)} %copy.9), calls=%async_computation | async-start | bytes 8388608 | tf_op jit(solution)/shard_map/all_to_all | solution.py:31
  437.1 108.6 %all-reduce.5.cloned.1.call-start = ((), (), s32[]{:S(2)}) async-start(), calls=%async_computation.4 | async-start | bytes 4194304 | tf_op jit(solution)/shard_map/psum | solution.py:30
Sparse Core Ops, SparseCore 0:
  9.2 299.6 all-gather.1
  330.1 96.4 all-reduce.2
  428.9 36.0 reduce-scatter.1
  468.0 77.6 all-reduce.4
where the time goes:
time: 559 us; the launch traced here: 558 us
  waiting for transfers between devices  470 us (84%)
  matrix products  59.1 us (11%)
  between operations  13.2 us (2%)
  local copies, waits for them, and re-layouts  10.8 us (2%)
    all_gather x1, waiting for transfers between devices, shards(): fragment = lax.all_gather(weights, 'col', axis=2, tiled=True)  302 us
    psum x1, waiting for transfers between devices, shards(): exposure = lax.psum(joined[:, :factor_cols, :], 'row')  75.1 us
    all_to_all x1, waiting for transfers between devices, shards(): lax.all_to_all(exposure, 'col', split_axis=2, concat_axis=1, tiled=True)  47.9 us
    psum x1, waiting for transfers between devices, shards(): left = lax.psum(left_part, 'col')  44.7 us
    dot_general x1, matrix products, shards(): jnp.einsum('dak,dap->dkp', weighted, fragment, preferred_element_type=jnp...  21.5 us
    dot_general x1, matrix products, shards(): jnp.einsum('dar,dap->drp', loadings, fragment, preferred_element_type=jnp...  21.1 us
  transfers between devices with their start and end apart: 5, of which 4 were waited for; matrix products, arithmetic and copies ran while one was open for 8% of the time, Pallas kernels for 0%

commit v1 on v0

--- a/solution.py
+++ b/solution.py
@@ -27,7 +27,8 @@
     left_part = jnp.einsum(
         "dri,drs->dis", exposure_rows, factor_cov, precision=lax.Precision.HIGHEST
     )
-    left = lax.psum(left_part, "col")
+    parts = lax.all_gather(left_part, "col")
+    left = jnp.sum(parts, axis=0)
     exposure_cols = lax.all_to_all(exposure, "col", split_axis=2, concat_axis=1, tiled=True)
     factor_block = jnp.einsum("dir,drk->dik", left, exposure_cols, precision=lax.Precision.HIGHEST)
     return factor_block + jnp.swapaxes(specific_block, 1, 2)

time: 559 us -> 614 us (1.098)
  blocking collectives: 0 us -> 93.3 us
  waiting for transfers between devices: 470 us -> 432 us
    all_to_all x0 -> x1, blocking collectives: none -> 93.3 us  [shards(): lax.all_to_all(exposure, 'col', split_axis=2, concat_axis=1, tiled=True)]
    all_to_all x1 -> x0, waiting for transfers between devices: 47.9 us -> none  [shards(): lax.all_to_all(exposure, 'col', split_axis=2, concat_axis=1, tiled=True)]
    psum x1 -> x0, waiting for transfers between devices: 44.7 us -> none  [shards(): left = lax.psum(left_part, 'col')]
    reduce_scatter x1, waiting for transfers between devices: 0.01 us -> 32.9 us  [shards(): lax.psum_scatter(joined[:, factor_cols:, :], 'row', scatter_dimension=2,...]
    psum x1, waiting for transfers between devices: 75.1 us -> 96.6 us  [shards(): exposure = lax.psum(joined[:, :factor_cols, :], 'row')]
  transfers between devices with their start and end apart: 5 -> 4, of which waited for: 4 -> 3; matrix products, arithmetic and copies ran while one was open for 8% -> 6% of each run, Pallas kernels for 0% -> 0%
where the time goes in v1:
time: 614 us; the launch traced here: 613 us
  waiting for transfers between devices  432 us (70%)
  blocking collectives  93.3 us (15%)
  matrix products  59.6 us (10%)
  between operations  13.2 us (2%)
  local copies, waits for them, and re-layouts  10.8 us (2%)
    all_gather x1, waiting for transfers between devices, shards(): fragment = lax.all_gather(weights, 'col', axis=2, tiled=True)  302 us
    psum x1, waiting for transfers between devices, shards(): exposure = lax.psum(joined[:, :factor_cols, :], 'row')  96.6 us
    all_to_all x1, blocking collectives, shards(): lax.all_to_all(exposure, 'col', split_axis=2, concat_axis=1, tiled=True)  93.3 us
    reduce_scatter x1, waiting for transfers between devices, shards(): lax.psum_scatter(joined[:, factor_cols:, :], 'row', scatter_dimension=2,...  32.9 us
    dot_general x1, matrix products, shards(): jnp.einsum('dak,dap->dkp', weighted, fragment, preferred_element_type=jnp...  22.5 us
    dot_general x1, matrix products, shards(): jnp.einsum('dar,dap->drp', loadings, fragment, preferred_element_type=jnp...  21.2 us
  transfers between devices with their start and end apart: 4, of which 3 were waited for; matrix products, arithmetic and copies ran while one was open for 6% of the time, Pallas kernels for 0%

profile of v1, /device:TPU:0, one launch (start us, length us, event | category | flops | bytes accessed | tf_op | source)
XLA Modules:
  0.0 613.5 jit_solution(17636186278484013295)
XLA Ops:
  6.5 0.0 all-gather.4.cloned.1.call-start
  6.5 0.7 all-gather.4.cloned.1.call-update
  7.3 0.0 all-reduce.2.cloned.1.call-start
  7.3 301.6 %all-gather.4.cloned.1.call-done = bf16[8,4096,512]{2,1,0:T(8,128)(2,1)} async-done(((bf16[8,4096,128]{2,1,0:T(8,128)(2,1)}), bf16[8,4096,512]{2,1,0:T(8,128)(2,1)}) %all-gather.4.cloned.1.call-update) | async-done | bytes 33554448 | tf_op jit(solution)/shard_map/all_gather | solution.py:14
  308.9 21.2 %fusion.5 = f32[8,256,512]{2,1,0:T(8,128)} fusion(bf16[8,4096,256]{2,1,0:T(8,128)(2,1)} %param.4, bf16[8,4096,512]{2,1,0:T(8,128)(2,1)} %all-gather.4.cloned.1.call-done), kind=kOutput, calls=%fused_computation.7 | convolution fusion | flops 8589934592 | bytes 54525952 | tf_op jit(solution)/shard_map/dar,dap->drp/dot_general | solution.py:15
  330.0 0.0 copy-start
  330.0 0.0 all-reduce.2.cloned.1.call-update
  330.1 0.0 all-gather.6.cloned.1.call-start
  330.1 96.6 %all-reduce.2.cloned.1.call-done = f32[8,256,512]{2,1,0:T(8,128)} async-done(((f32[8,256,512]{2,1,0:T(8,128)}), f32[8,256,512]{2,1,0:T(8,128)}) %all-reduce.2.cloned.1.call-update) | async-done | bytes 4194320 | tf_op jit(solution)/shard_map/psum | solution.py:22
  426.7 10.4 %fusion.2 = f32[8,64,1024]{2,1,0:T(8,128)} fusion(f32[8,256,1024]{2,1,0:T(8,128)} %param.7, f32[8,256,512]{2,1,0:T(8,128)} %all-reduce.2.cloned.1.call-done, s32[]{:T(128)S(6)} %select_n.3), kind=kOutput, calls=%fused_computation.4 | convolution fusion | flops 1610612736 | bytes 11534340 | tf_op jit(solution)/shard_map/dri,drs->dis/dot_general | solution.py:27
  437.2 0.0 all-gather.6.cloned.1.call-update
  437.2 0.2 reduce-scatter.2.cloned.1.call-start
  437.4 0.0 copy-done
  437.4 22.5 %fusion = f32[8,128,512]{1,2,0:T(8,128)} fusion(bf16[8,4096,512]{2,1,0:T(8,128)(2,1)} %all-gather.4.cloned.1.call-done, bf16[8,4096,128]{2,1,0:T(8,128)(2,1)} %param.5, f32[8,4096]{1,0:T(8,128)S(1)} %copy-done), kind=kOutput, calls=%fused_computation.1 | convolution fusion | flops 4307550208 | bytes 44171264 | tf_op jit(solution)/shard_map/dak,dap->dkp/dot_general | solution.py:18
  459.9 0.0 reduce-scatter.2.cloned.1.call-update
  459.9 5.4 copy.11
  465.4 93.3 %all_to_all.18 = f32[8,256,512]{1,0,2:T(8,128)} all-to-all(f32[8,256,512]{1,0,2:T(8,128)} %copy.11), channel_id=1, replica_groups=mesh['row'=8,'col'=4] {'col'}, dimensions={2} | all-to-all | bytes 8388608 | tf_op jit(solution)/shard_map/all_to_all | solution.py:32
  558.6 5.3 copy.12
  563.9 0.0 all-gather.6.cloned.1.call-done
  563.9 4.6 reduce_sum.9
  568.5 32.9 %reduce-scatter.2.cloned.1.call-done = f32[8,128,64]{1,2,0:T(8,128)} async-done(((f32[8,128,512]{1,2,0:T(8,128)}), f32[8,128,64]{1,2,0:T(8,128)}) %reduce-scatter.2.cloned.1.call-update) | async-done | bytes 262160 | tf_op jit(solution)/shard_map/reduce_scatter | solution.py:23
  601.4 5.5 convolution_add_fusion
Async XLA Ops:
  6.5 302.3 %all-gather.4.cloned.1.call-start = ((), (), s32[]{:S(2)}) async-start(), calls=%async_computation.2 | async-start | bytes 41943040 | tf_op jit(solution)/shard_map/all_gather | solution.py:14
  7.3 419.5 %all-reduce.2.cloned.1.call-start = ((), (), s32[]{:S(2)}) async-start(), calls=%async_computation.3 | async-start | bytes 8388608 | tf_op jit(solution)/shard_map/psum | solution.py:22
  330.0 107.4 %copy-start = (f32[8,4096]{1,0:T(8,128)S(1)}, f32[8,4096]{1,0:T(8,128)}, u32[]{:S(2)}) copy-start(f32[8,4096]{1,0:T(8,128)} %param.6) | copy-start | bytes 393220
  330.1 233.9 %all-gather.6.cloned.1.call-start = ((), (), s32[]{:S(2)}) async-start(), calls=%async_computation.5 | async-start | bytes 10485760 | tf_op jit(solution)/shard_map/all_gather | solution.py:30
  437.2 164.3 %reduce-scatter.2.cloned.1.call-start = ((), (), s32[]{:S(2)}) async-start(), calls=%async_computation.4 | async-start | bytes 2359296 | tf_op jit(solution)/shard_map/reduce_scatter | solution.py:23
Sparse Core Ops, SparseCore 0:
  9.2 299.6 all-gather.3
  330.2 96.4 all-reduce.1
  437.3 126.4 all-gather.5
  565.9 35.4 reduce-scatter.1

commit v2 on v0

--- a/solution.py
+++ b/solution.py
@@ -2,6 +2,11 @@
 import jax.numpy as jnp
 from jax import lax
 from jax.sharding import PartitionSpec as P
+
+
+def all_parts(x, axis, dim):
+    pieces = lax.all_gather(x, axis)
+    return jnp.concatenate(pieces, axis=dim)
 
 
 def shards(loadings, weights, specific, factor_cov):
@@ -11,7 +16,7 @@
     port_rows = total_ports // lax.axis_size("row")
     row_start = lax.axis_index("row") * port_rows
     weighted = (specific[:, :, None] * weights.astype(jnp.float32)).astype(jnp.bfloat16)
-    fragment = lax.all_gather(weights, "col", axis=2, tiled=True)
+    fragment = all_parts(weights, "col", 2)
     exposure_part = jnp.einsum(
         "dar,dap->drp", loadings, fragment, preferred_element_type=jnp.float32
     )

time: 559 us -> 673 us (1.20)
  local copies, waits for them, and re-layouts: 10.8 us -> 97.3 us
  blocking collectives: 0 us -> 70.4 us
  waiting for transfers between devices: 470 us -> 431 us
    all_to_all x0 -> x1, blocking collectives: none -> 70.4 us  [shards(): lax.all_to_all(exposure, 'col', split_axis=2, concat_axis=1, tiled=True)]
    reshape x0 -> x1, local copies, waits for them, and re-layouts: none -> 48.5 us  [all_parts(): return jnp.concatenate(pieces, axis=dim)]
    all_to_all x1 -> x0, waiting for transfers between devices: 47.9 us -> none  [shards(): lax.all_to_all(exposure, 'col', split_axis=2, concat_axis=1, tiled=True)]
    psum x1, waiting for transfers between devices: 44.7 us -> 0.01 us  [shards(): left = lax.psum(left_part, 'col')]
    all_gather x0 -> x1, local copies, waits for them, and re-layouts: none -> 38 us  [all_parts(): pieces = lax.all_gather(x, axis)]
    reduce_scatter x1, waiting for transfers between devices: 0.01 us -> 31.7 us  [shards(): lax.psum_scatter(joined[:, factor_cols:, :], 'row', scatter_dimension=2,...]
    psum x1, waiting for transfers between devices: 75.1 us -> 96.6 us  [shards(): exposure = lax.psum(joined[:, :factor_cols, :], 'row')]
  transfers between devices with their start and end apart: 5 -> 4, of which waited for: 4 -> 3; matrix products, arithmetic and copies ran while one was open for 8% -> 5% of each run, Pallas kernels for 0% -> 0%
where the time goes in v2:
time: 673 us; the launch traced here: 671 us
  waiting for transfers between devices  431 us (64%)
  local copies, waits for them, and re-layouts  97.3 us (14%)
  blocking collectives  70.4 us (10%)
  matrix products  59 us (9%)
  between operations  13.1 us (2%)
    all_gather x1, waiting for transfers between devices, all_parts(): pieces = lax.all_gather(x, axis)  302 us
    psum x1, waiting for transfers between devices, shards(): exposure = lax.psum(joined[:, :factor_cols, :], 'row')  96.6 us
    all_to_all x1, blocking collectives, shards(): lax.all_to_all(exposure, 'col', split_axis=2, concat_axis=1, tiled=True)  70.4 us
    reshape x1, local copies, waits for them, and re-layouts, all_parts(): return jnp.concatenate(pieces, axis=dim)  48.5 us
    all_gather x1, local copies, waits for them, and re-layouts, all_parts(): pieces = lax.all_gather(x, axis)  38 us
    reduce_scatter x1, waiting for transfers between devices, shards(): lax.psum_scatter(joined[:, factor_cols:, :], 'row', scatter_dimension=2,...  31.7 us
    dot_general x1, matrix products, shards(): jnp.einsum('dak,dap->dkp', weighted, fragment, preferred_element_type=jnp...  21.4 us
    dot_general x1, matrix products, shards(): jnp.einsum('dar,dap->drp', loadings, fragment, preferred_element_type=jnp...  21.1 us
  transfers between devices with their start and end apart: 4, of which 3 were waited for; matrix products, arithmetic and copies ran while one was open for 5% of the time, Pallas kernels for 0%

profile of v2, /device:TPU:0, one launch (start us, length us, event | category | flops | bytes accessed | tf_op | source)
XLA Modules:
  0.0 671.0 jit_solution(3566894460127536789)
XLA Ops:
  6.5 0.0 all-gather.3.cloned.1.call-start
  6.5 0.7 all-gather.3.cloned.1.call-update
  7.3 0.0 all-reduce.3.cloned.1.call-start
  7.3 301.7 %all-gather.3.cloned.1.call-done = bf16[32,4096,128]{2,1,0:T(8,128)(2,1)} async-done(((bf16[8,4096,128]{2,1,0:T(8,128)(2,1)}), bf16[32,4096,128]{2,1,0:T(8,128)(2,1)}) %all-gather.3.cloned.1.call-update) | async-done | bytes 33554448 | tf_op jit(solution)/shard_map/all_gather | solution.py:8
  309.0 38.0 %copy.17 = bf16[4,8,4096,128]{3,0,2,1:T(4,128)(2,1)} copy(bf16[4,8,4096,128]{3,2,1,0:T(8,128)(2,1)} %bitcast.17) | data formatting | bytes 67108864 | tf_op jit(solution)/shard_map/all_gather | solution.py:8
  347.0 48.5 %reshape.8 = bf16[8,4096,512]{2,1,0:T(8,128)(2,1)} reshape(bf16[8,4096,4,128]{3,2,1,0:T(4,128)(2,1)} %bitcast.16) | data formatting | bytes 67108864 | tf_op jit(solution)/shard_map/reshape | solution.py:9
  395.5 21.1 %fusion.5 = f32[8,256,512]{2,1,0:T(8,128)} fusion(bf16[8,4096,256]{2,1,0:T(8,128)(2,1)} %param.4, bf16[8,4096,512]{2,1,0:T(8,128)(2,1)} %reshape.8), kind=kOutput, calls=%fused_computation.8 | convolution fusion | flops 8589934592 | bytes 54525952 | tf_op jit(solution)/shard_map/dar,dap->drp/dot_general | solution.py:20
  416.6 0.0 copy-start
  416.6 0.0 all-reduce.3.cloned.1.call-update
  416.6 0.0 all-reduce.5.cloned.1.call-start
  416.7 96.6 %all-reduce.3.cloned.1.call-done = f32[8,256,512]{2,1,0:T(8,128)} async-done(((f32[8,256,512]{2,1,0:T(8,128)}), f32[8,256,512]{2,1,0:T(8,128)}) %all-reduce.3.cloned.1.call-update) | async-done | bytes 4194320 | tf_op jit(solution)/shard_map/psum | solution.py:27
  513.3 10.4 %fusion.2 = f32[8,64,1024]{2,1,0:T(8,128)} fusion(f32[8,256,1024]{2,1,0:T(8,128)} %param.7, f32[8,256,512]{2,1,0:T(8,128)} %all-reduce.3.cloned.1.call-done, s32[]{:T(128)S(6)} %select_n.3), kind=kOutput, calls=%fused_computation.5 | convolution fusion | flops 1610612736 | bytes 11534340 | tf_op jit(solution)/shard_map/dri,drs->dis/dot_general | solution.py:32
  523.7 0.0 all-reduce.5.cloned.1.call-update
  523.7 0.2 reduce-scatter.2.cloned.1.call-start
  523.9 0.0 copy-done
  523.9 21.4 %fusion = f32[8,128,512]{1,2,0:T(8,128)} fusion(bf16[8,4096,512]{2,1,0:T(8,128)(2,1)} %reshape.8, bf16[8,4096,128]{2,1,0:T(8,128)(2,1)} %param.5, f32[8,4096]{1,0:T(8,128)S(1)} %copy-done), kind=kOutput, calls=%fused_computation.2 | convolution fusion | flops 4307550208 | bytes 44171264 | tf_op jit(solution)/shard_map/dak,dap->dkp/dot_general | solution.py:23
  545.3 0.0 reduce-scatter.2.cloned.1.call-update
  545.4 5.4 copy.11
  550.8 70.4 %all_to_all.18 = f32[8,256,512]{1,0,2:T(8,128)} all-to-all(f32[8,256,512]{1,0,2:T(8,128)} %copy.11), channel_id=1, replica_groups=mesh['row'=8,'col'=4] {'col'}, dimensions={2} | all-to-all | bytes 8388608 | tf_op jit(solution)/shard_map/all_to_all | solution.py:36
  621.2 5.3 copy.12
  626.6 0.0 all-reduce.5.cloned.1.call-done
  626.6 31.7 %reduce-scatter.2.cloned.1.call-done = f32[8,128,64]{1,2,0:T(8,128)} async-done(((f32[8,128,512]{1,2,0:T(8,128)}), f32[8,128,64]{1,2,0:T(8,128)}) %reduce-scatter.2.cloned.1.call-update) | async-done | bytes 262160 | tf_op jit(solution)/shard_map/reduce_scatter | solution.py:28
  658.2 6.2 convolution_add_fusion
Async XLA Ops:
  6.5 302.5 %all-gather.3.cloned.1.call-start = ((), (), s32[]{:S(2)}) async-start(), calls=%async_computation.5 | async-start | bytes 41943040 | tf_op jit(solution)/shard_map/all_gather | solution.py:8
  7.3 506.0 %all-reduce.3.cloned.1.call-start = ((), (), s32[]{:S(2)}) async-start(), calls=%async_computation.2 | async-start | bytes 8388608 | tf_op jit(solution)/shard_map/psum | solution.py:27
  416.6 107.3 %copy-start = (f32[8,4096]{1,0:T(8,128)S(1)}, f32[8,4096]{1,0:T(8,128)}, u32[]{:S(2)}) copy-start(f32[8,4096]{1,0:T(8,128)} %param.6) | copy-start | bytes 393220
  416.6 209.9 %all-reduce.5.cloned.1.call-start = ((), (), s32[]{:S(2)}) async-start(), calls=%async_computation.3 | async-start | bytes 4194304 | tf_op jit(solution)/shard_map/psum | solution.py:35
  523.7 134.5 %reduce-scatter.2.cloned.1.call-start = ((), (), s32[]{:S(2)}) async-start(), calls=%async_computation.4 | async-start | bytes 2359296 | tf_op jit(solution)/shard_map/reduce_scatter | solution.py:28
Sparse Core Ops, SparseCore 0:
  9.2 299.7 all-gather.2
  416.7 96.4 all-reduce.2
  523.8 96.3 all-reduce.4
  622.3 35.8 reduce-scatter.1
